TPU v7x, 32 devices: a whole 2x2x4 slice. The times are simulated.
32 devices in a mesh: tm: 4 (over y, x), space: 8 (over z, core).
Axes of the slice: x: 2, y: 2, z: 4, core: 2. Of those that a mesh axis runs over, the one named last changes fastest.
Arguments:
- hidden_in: bfloat16 [8, 16, 32, 5120], P('tm', 'space'), may hold values from -6 to 6
- queries: bfloat16 [8, 16, 32, 5120], P('tm', 'space'), may hold values from -250 to 250
- keys: bfloat16 [8, 16, 32, 5120], P('tm', 'space'), may hold values from -250 to 250
- values: bfloat16 [8, 16, 32, 5120], P('tm', 'space'), may hold values from -6 to 6
- query_gain: float32 [5120], replicated, may hold values from 0.5 to 3
- key_gain: float32 [5120], replicated, may hold values from 0.5 to 3
- reach_time: int32 [40], replicated, may hold values from 0 to 1
- reach_rows: int32 [40], replicated, may hold values from 0 to 1
- reach_cols: int32 [40], replicated, may hold values from 0 to 2
- out_weight: bfloat16 [5120, 5120], P('space', 'tm'), may hold values from -0.25 to 0.25
- gate: float32 [5120], replicated, may hold values from -1.5 to 1.5
Outputs:
- output: bfloat16 [8, 16, 32, 5120], P('tm', 'space')
All inputs are finite; a program needn't handle non-finite values.
Results may differ from a plain program's by a relative error of at most 0.013.
The roundings to bfloat16 on the way count: a program that leaves them out, or rounds other values in their place, can miss the bound.
Values may be sent and summed in bfloat16 or wider, within the bound.
A program may use at most 128 MiB of HBM per device.

v0:
```python
import functools
import math

import jax
import jax.numpy as jnp
import numpy as np
from jax import lax
from jax.experimental import pallas as pl
from jax.experimental.pallas import tpu as pltpu
from jax.sharding import PartitionSpec as P

TW = 8
REACHES = [(a, b, c) for a in range(2) for b in range(2) for c in range(3)]


def normalized(source, gain):
    values_f = source.astype(jnp.float32)
    mean_square = jnp.mean(values_f * values_f, axis=-1, keepdims=True)
    return (values_f * lax.rsqrt(mean_square + 1e-06) * gain).astype(jnp.bfloat16)


def places(frames, rows, columns, margin):
    grid = np.meshgrid(
        np.arange(-margin, frames + margin),
        np.arange(-margin, rows + margin),
        np.arange(columns) // TW,
        indexing="ij",
    )
    return np.stack([axis.reshape(-1) for axis in grid]).astype(np.int32)


def kernel(
    heads,
    group,
    time_ref,
    rows_ref,
    cols_ref,
    raw_query_ref,
    key_ref,
    query_gain_ref,
    key_gain_ref,
    query_place_ref,
    key_place_ref,
    gate_ref,
    value_ref,
    weight_ref,
    hidden_in_ref,
    out_ref,
    query_ref,
    mask_ref,
    hidden_ref,
    region,
    weights,
    mixed,
    total,
    outgoing,
    incoming,
    local_sem,
    own_sem,
    halo_send,
    halo_recv,
    near_send,
    pair_send,
    weight_recv,
    mixed_send,
    mixed_recv,
    back_send,
    back_recv,
):
    t = lax.axis_index("tm")
    s = lax.axis_index("space")
    nt = lax.axis_size("tm")
    ns = lax.axis_size("space")
    chips = ns // 2
    frames, rows, columns, inner = value_ref.shape
    tokens = frames * rows * columns
    keys_here = (frames + 2) * (rows + 2) * columns
    width = inner // heads
    depth, cols = weight_ref.shape

    def remote(source, target, send, recv, tm, space):
        return pltpu.make_async_remote_copy(
            src_ref=source,
            dst_ref=target,
            send_sem=send,
            recv_sem=recv,
            device_id=(tm, space),
            device_id_type=pl.DeviceIdType.MESH,
        )

    has_low_t, has_high_t = t > 0, t < nt - 1
    has_low_s, has_high_s = s > 0, s < ns - 1
    own_f, own_r = pl.ds(1, frames), pl.ds(1, rows)

    def halo(i, source, target, tm, space):
        return remote(source, target, halo_send.at[i], halo_recv.at[i], tm, space)

    straight = []
    for part, whole in ((1, value_ref), (0, region.at[0, own_f, own_r])):
        straight += [
            (halo(4 * part, whole.at[frames - 1], region.at[part, 0, own_r], t + 1, s), has_high_t, has_low_t),
            (halo(4 * part + 1, whole.at[0], region.at[part, frames + 1, own_r], t - 1, s), has_low_t, has_high_t),
            (halo(4 * part + 2, whole.at[:, rows - 1], region.at[part, own_f, 0], t, s + 1), has_high_s, has_low_s),
            (halo(4 * part + 3, whole.at[:, 0], region.at[part, own_f, rows + 1], t, s - 1), has_low_s, has_high_s),
        ]
    corners = []
    for i, (frame, has_frame) in enumerate(((0, has_low_t), (frames + 1, has_high_t))):
        corners.append((
            halo(8 + 2 * i, region.at[:, frame, rows], region.at[:, frame, 0], t, s + 1),
            has_frame & has_high_s, has_frame & has_low_s,
        ))
        corners.append((
            halo(9 + 2 * i, region.at[:, frame, 1], region.at[:, frame, rows + 1], t, s - 1),
            has_frame & has_low_s, has_frame & has_high_s,
        ))
    parts, lane = weights.shape[0], weights.shape[2]

    def block(b, p):
        return weights.at[p, pl.ds(pl.multiple_of(b * depth, depth), depth)]

    def own_block(p):
        return weight_ref.at[:, pl.ds(pl.multiple_of(p * lane, lane), lane)]

    partner = s + 1 - 2 * lax.rem(s, 2)

    def near(k, b, way, p, first):
        space = s + 2 if way == 0 else s - 2
        source = own_block(p) if first else block(b, p)
        return remote(source, block(b, p), near_send.at[way, k, p], weight_recv.at[b, p], t, space)

    def pair(k, b, way, p, first):
        source = own_block(p) if first else block(b, p)
        return remote(source, block(b, p), pair_send.at[way, k, p], weight_recv.at[b, p], t, partner)

    def arrived(b, p):
        remote(block(b, p), block(b, p), pair_send.at[0, 0, p], weight_recv.at[b, p], t, partner).wait_recv()

    def each_part(low, high, run):
        def body(p, carry):
            run(p)
            return carry

        lax.fori_loop(low, high, body, 0)

    for copy, sends, _ in straight[:4]:
        pl.when(sends)(copy.start)

    def first_part(p):
        pl.when(s + 2 < ns)(near(0, s, 0, p, True).start)
        pl.when(s >= 2)(near(0, s, 1, p, True).start)
        pair(0, s, 0, p, True).start()
        pltpu.make_async_copy(own_block(p), block(s, p), own_sem.at[p]).start()

    each_part(0, parts, first_part)
    own_value = pltpu.make_async_copy(value_ref, region.at[1, own_f, own_r], local_sem.at[0])
    own_value.start()
    own_hidden = pltpu.make_async_copy(hidden_in_ref, hidden_ref, local_sem.at[1])
    own_hidden.start()

    step = 16 if columns % 16 == 0 else columns
    for frame in range(frames):
        for row in range(rows):
            for column in range(0, columns, step):
                at = slice(column, column + step)
                region[0, 1 + frame, 1 + row, at] = normalized(key_ref[frame, row, at], key_gain_ref[...])

    def query_rows(i, carry):
        at = pl.ds(pl.multiple_of(i * 16, 16), 16)
        query_ref[at] = normalized(raw_query_ref[at], query_gain_ref[...])
        return carry

    lax.fori_loop(0, tokens // 16, query_rows, 0)
    for copy, sends, _ in straight[4:]:
        pl.when(sends)(copy.start)

    def clear_frame(frame):
        def run():
            for part in range(2):
                for row in range(rows + 2):
                    region[part, frame, row] = jnp.zeros((columns, inner), jnp.bfloat16)
        return run

    def clear_row(row):
        def run():
            for part in range(2):
                for frame in range(frames + 2):
                    region[part, frame, row] = jnp.zeros((columns, inner), jnp.bfloat16)
        return run

    pl.when(jnp.logical_not(has_low_t))(clear_frame(0))
    pl.when(jnp.logical_not(has_high_t))(clear_frame(frames + 1))
    pl.when(jnp.logical_not(has_low_s))(clear_row(0))
    pl.when(jnp.logical_not(has_high_s))(clear_row(rows + 1))

    frame_k, row_k, tile_k = key_place_ref[0:1], key_place_ref[1:2], key_place_ref[2:3]
    inside = (frame_k >= -t * frames) & (frame_k < (nt - t) * frames)
    inside = inside & (row_k >= -s * rows) & (row_k < (ns - s) * rows)
    outside = jnp.where(inside, 0, 9)
    frame_gap = jnp.abs(query_place_ref[:, 0:1] - frame_k) + outside
    row_gap = jnp.abs(query_place_ref[:, 1:2] - row_k)
    tile_gap = jnp.abs(query_place_ref[:, 2:3] - tile_k)
    for i, (reach_t, reach_r, reach_c) in enumerate(REACHES):
        allowed = (frame_gap <= reach_t) & (row_gap <= reach_r) & (tile_gap <= reach_c)
        mask_ref[i] = jnp.where(allowed, 0.0, -1e30)

    def relay(k, p):
        low, high = s - 2 * k, s + 2 * k

        @pl.when(low >= 0)
        def _():
            arrived(low, p)
            pl.when(s + 2 < ns)(near(k, low, 0, p, False).start)
            pair(k, low, 0, p, False).start()

        @pl.when(high < ns)
        def _():
            arrived(high, p)
            pl.when(s >= 2)(near(k, high, 1, p, False).start)
            pair(k, high, 1, p, False).start()

    def relay_parts(k, low, high):
        if 1 <= k < chips:
            each_part(low, high, functools.partial(relay, k))

    early = parts // 2
    last = chips - 1
    if last > 1:
        relay_parts(1, 0, early)
    for copy, _, receives in straight[0:2] + straight[4:6]:
        pl.when(receives)(copy.wait_recv)
    for copy, sends, _ in corners:
        pl.when(sends)(copy.start)
    for copy, _, receives in straight[2:4] + straight[6:8]:
        pl.when(receives)(copy.wait_recv)
    for copy, _, receives in corners:
        pl.when(receives)(copy.wait_recv)
    if last > 1:
        relay_parts(1, early, parts)
    own_value.wait()

    groups = heads // group
    span = group * width

    def gather(g, d):
        at = (t, slice(None), pl.ds(pl.multiple_of(g * span, span), span))
        return remote(
            mixed.at[at], mixed.at[at], mixed_send.at[d - 1, g], mixed_recv.at[t, g],
            lax.rem(t + d, nt), s,
        )

    def one_group(g, carry):
        for i in range(group):
            h = g * group + i
            lanes = pl.ds(pl.multiple_of(h * width, width), width)
            query = query_ref[:, lanes]
            key = region[0, :, :, :, lanes].reshape(keys_here, width)
            value = region[1, :, :, :, lanes].reshape(keys_here, width)
            scores = lax.dot_general(
                query, key, (((1,), (1,)), ((), ())), preferred_element_type=jnp.float32
            ) * width ** (-0.5)
            scores = scores + mask_ref[time_ref[h] * 6 + rows_ref[h] * 3 + cols_ref[h]]
            part = jnp.exp(scores - jnp.max(scores, axis=1, keepdims=True))
            sums = jnp.sum(part, axis=1, keepdims=True)
            result = jnp.dot(part.astype(jnp.bfloat16), value, preferred_element_type=jnp.float32)
            mixed[t, :, lanes] = (result / sums).astype(jnp.bfloat16)
        for d in range(1, nt):
            gather(g, d).start()
        return carry

    ahead = groups * 5 // 8
    lax.fori_loop(0, ahead, one_group, 0)
    if last > 2:
        relay_parts(2, 0, parts)
    lax.fori_loop(ahead, groups, one_group, 0)
    for k in range(3, last):
        relay_parts(k, 0, parts)

    def gathered(g, carry):
        for d in range(1, nt):
            other = lax.rem(t + d, nt)
            at = (other, slice(None), pl.ds(pl.multiple_of(g * span, span), span))
            remote(mixed.at[at], mixed.at[at], mixed_send.at[d - 1, g], mixed_recv.at[other, g], t, s).wait_recv()
        return carry

    chip_depth = 2 * depth
    piece = chip_depth * 128 // math.gcd(chip_depth, 128)

    def multiply(start, p, first):
        feature = pl.ds(pl.multiple_of(start, piece), piece)
        left = mixed[:, :, feature].reshape(nt * tokens, piece)
        product = jnp.dot(left, weights[p, feature], preferred_element_type=jnp.float32)
        if first:
            total[p] = product
        else:
            total[p] += product

    chip = s // 2
    half = lax.rem(s, 2)

    def add(k, p):
        for other in (chip - k, chip + k):
            @pl.when((other >= 0) & (other < chips))
            def _():
                arrived(2 * other + 1 - half, p)
                multiply(other * piece, p, False)

    def own_rows(owner):
        return pl.ds(pl.multiple_of(owner * tokens, tokens), tokens)

    def back(d, p):
        other = lax.rem(t + d, nt)
        return remote(
            outgoing.at[d - 1, p], incoming.at[d - 1, p], back_send.at[d - 1, p], back_recv.at[d - 1, p], other, s
        )

    def send_back(p):
        for d in range(1, nt):
            outgoing[d - 1, p] = total[p, own_rows(lax.rem(t + d, nt)), :].astype(jnp.bfloat16)
            back(d, p).start()

    def own_part(p):
        pltpu.make_async_copy(own_block(p), block(s, p), own_sem.at[p]).wait()
        arrived(partner, p)

    lax.fori_loop(0, groups, gathered, 0)
    if piece == chip_depth:
        def begin(p):
            own_part(p)
            multiply(chip * piece, p, True)
            for k in range(1, last):
                add(k, p)

        each_part(0, parts, begin)

        def conclude(p):
            if last > 0:
                relay(last, p)
                add(last, p)
            send_back(p)

        each_part(0, parts, conclude)
    else:
        def conclude(p):
            own_part(p)
            if last > 0:
                relay(last, p)
            for k in range(1, chips):
                for other in (chip - k, chip + k):
                    @pl.when((other >= 0) & (other < chips))
                    def _():
                        arrived(2 * other + 1 - half, p)
            multiply(0, p, True)

            def add_piece(i, carry):
                multiply(i * piece, p, False)
                return carry

            lax.fori_loop(1, inner // piece, add_piece, 0)
            send_back(p)

        each_part(0, parts, conclude)

    own_hidden.wait()

    def finish(owner, p, branch):
        lanes = pl.ds(pl.multiple_of(owner * cols + p * lane, lane), lane)
        out_ref[:, lanes] = (
            hidden_ref[:, lanes].astype(jnp.float32) + gate_ref[:, lanes] * branch
        ).astype(jnp.bfloat16)

    def finish_own(p):
        finish(t, p, total[p, own_rows(t), :])

    def finish_others(p):
        for d in range(1, nt):
            back(d, p).wait_recv()
            finish(lax.rem(t + nt - d, nt), p, incoming[d - 1, p].astype(jnp.float32))

    each_part(0, parts, finish_own)
    each_part(0, parts, finish_others)

    for copy, sends, _ in straight + corners:
        pl.when(sends)(copy.wait_send)
    for k in range(chips):
        low, high = s - 2 * k, s + 2 * k

        def weight_sent(p):
            pl.when((low >= 0) & (s + 2 < ns))(near(k, low, 0, p, k == 0).wait_send)
            pl.when((high < ns) & (s >= 2))(near(k, high, 1, p, k == 0).wait_send)
            pl.when(low >= 0)(pair(k, low, 0, p, k == 0).wait_send)
            if k > 0:
                pl.when(high < ns)(pair(k, high, 1, p, False).wait_send)

        each_part(0, parts, weight_sent)

    def sent(g, carry):
        for d in range(1, nt):
            gather(g, d).wait_send()
        return carry

    lax.fori_loop(0, groups, sent, 0)

    def back_sent(p):
        for d in range(1, nt):
            back(d, p).wait_send()

    each_part(0, parts, back_sent)


def shards(
    hidden_in,
    queries,
    keys,
    values,
    query_gain,
    key_gain,
    reach_time,
    reach_rows,
    reach_cols,
    out_weight,
    gate,
):
    frames, rows, columns, inner = queries.shape
    width = hidden_in.shape[3]
    heads = reach_time.shape[0]
    tokens = frames * rows * columns
    nt, ns = lax.axis_size("tm"), lax.axis_size("space")
    depth, cols = out_weight.shape
    group = 5 if heads % 5 == 0 else 1
    vmem = pl.BlockSpec(memory_space=pltpu.VMEM)
    hbm = pl.BlockSpec(memory_space=pl.ANY)
    dma = pltpu.SemaphoreType.DMA
    lane = 256 if cols % 256 == 0 else 128
    parts = cols // lane
    output = pl.pallas_call(
        functools.partial(kernel, heads, group),
        out_shape=jax.ShapeDtypeStruct((tokens, width), jnp.bfloat16),
        in_specs=[pl.BlockSpec(memory_space=pltpu.SMEM)] * 3 + [vmem] * 7 + [hbm] * 3,
        out_specs=vmem,
        scratch_shapes=[
            pltpu.VMEM((tokens, inner), jnp.bfloat16),
            pltpu.VMEM((len(REACHES), tokens, (frames + 2) * (rows + 2) * columns), jnp.float32),
            pltpu.VMEM((tokens, width), jnp.bfloat16),
            pltpu.VMEM((2, frames + 2, rows + 2, columns, inner), jnp.bfloat16),
            pltpu.VMEM((parts, depth * ns, lane), jnp.bfloat16),
            pltpu.VMEM((nt, tokens, inner), jnp.bfloat16),
            pltpu.VMEM((parts, nt * tokens, lane), jnp.float32),
            pltpu.VMEM((nt - 1, parts, tokens, lane), jnp.bfloat16),
            pltpu.VMEM((nt - 1, parts, tokens, lane), jnp.bfloat16),
            dma((2,)),
            dma((parts,)),
            dma((12,)),
            dma((12,)),
            dma((2, ns // 2, parts)),
            dma((2, ns // 2, parts)),
            dma((ns, parts)),
            dma((nt - 1, heads // group)),
            dma((nt, heads // group)),
            dma((nt - 1, parts)),
            dma((nt - 1, parts)),
        ],
        compiler_params=pltpu.CompilerParams(
            has_side_effects=True, vmem_limit_bytes=60 * 1024 * 1024
        ),
    )(
        reach_time,
        reach_rows,
        reach_cols,
        queries.reshape(tokens, inner),
        keys,
        query_gain.reshape(1, inner),
        key_gain.reshape(1, inner),
        places(frames, rows, columns, 0).T,
        places(frames, rows, columns, 1),
        gate.reshape(1, width),
        values,
        out_weight,
        hidden_in.reshape(tokens, width),
    )
    return output.reshape(frames, rows, columns, width)


def solution(mesh):
    in_specs = (
        P("tm", "space", None, None),
        P("tm", "space", None, None),
        P("tm", "space", None, None),
        P("tm", "space", None, None),
        P(),
        P(),
        P(),
        P(),
        P(),
        P("space", "tm"),
        P(),
    )
    out_specs = P("tm", "space", None, None)
    return jax.shard_map(shards, mesh=mesh, in_specs=in_specs, out_specs=out_specs, check_vma=False)
```

profile of v0, /device:TPU:0, one launch (start us, length us, event | category | flops | bytes accessed | tf_op | source)
XLA Modules:
  0.0 168.5 jit_solution(66881350622307801)
XLA Ops:
  0.0 166.1 %shard_map.127 = bf16[128,5120]{1,0:T(8,128)(2,1)} custom-call(s32[40]{0:T(128)} %time_ref.1, s32[40]{0:T(128)} %rows_ref.1, s32[40]{0:T(128)} %cols_ref.1, bf16[128,5120]{1,0:T(8,128)(2,1)} %bitcast.7, bf16[2,2,32,5120]{3,2,1,0:T(8,128)(2,1)} %key_ref.1, f32[1,5120]{1,0:T(1,128)} %bitcast.9, f32[1,5120]{1,0:T(1,128)} %bitcast.10, ...), custom_call_target="tpu_custom_call" | custom-call | tf_op jit(solution)/shard_map/pallas_call | solution.py:435
  166.1 2.5 %copy.15 = bf16[2,2,32,5120]{3,2,1,0:T(8,128)(2,1)} copy(bf16[2,2,32,5120]{3,2,1,0:T(8,128)(2,1)} %bitcast.6) | data formatting | bytes 2621440
where the time goes:
time: 171 us; the launch traced here: 169 us
  Pallas kernels  166 us (97%)
  local copies, waits for them, and re-layouts  2.46 us (1%)
    pallas_call x1, Pallas kernels, shards(): pl.pallas_call(functools.partial(kernel, heads, group), out_shape=jax.Sha...  166 us

commit v1 on v0

--- a/solution.py
+++ b/solution.py
@@ -29,7 +29,7 @@
     return np.stack([axis.reshape(-1) for axis in grid]).astype(np.int32)
 
 
-def kernel(
+def ring_kernel(
     heads,
     group,
     time_ref,
@@ -407,7 +407,7 @@
     each_part(0, parts, back_sent)
 
 
-def shards(
+def ring_shards(
     hidden_in,
     queries,
     keys,
@@ -433,7 +433,7 @@
     lane = 256 if cols % 256 == 0 else 128
     parts = cols // lane
     output = pl.pallas_call(
-        functools.partial(kernel, heads, group),
+        functools.partial(ring_kernel, heads, group),
         out_shape=jax.ShapeDtypeStruct((tokens, width), jnp.bfloat16),
         in_specs=[pl.BlockSpec(memory_space=pltpu.SMEM)] * 3 + [vmem] * 7 + [hbm] * 3,
         out_specs=vmem,
@@ -480,6 +480,732 @@
     return output.reshape(frames, rows, columns, width)
 
 
+def pair_kernel(
+    heads,
+    time_ref,
+    rows_ref,
+    cols_ref,
+    query_gain_ref,
+    key_gain_ref,
+    query_place_ref,
+    key_place_ref,
+    gate_ref,
+    raw_query_ref,
+    raw_key_ref,
+    value_ref,
+    weight_ref,
+    hidden_in_ref,
+    out_ref,
+    raw,
+    normed,
+    region,
+    query_ref,
+    mask_ref,
+    mixed,
+    weights,
+    total,
+    partial_out,
+    partial_in,
+    outgoing,
+    incoming,
+    hidden_ref,
+    local_sem,
+    value_sem,
+    own_sem,
+    swap_send,
+    swap_recv,
+    side_send,
+    side_recv,
+    corner_send,
+    corner_recv,
+    near_send,
+    cross_send,
+    pair_send,
+    weight_recv,
+    level_send,
+    level_recv,
+    mixed_send,
+    mixed_recv,
+    part_send,
+    part_recv,
+    back_send,
+    back_recv,
+):
+    t = lax.axis_index("tm")
+    s = lax.axis_index("space")
+    nt = lax.axis_size("tm")
+    ns = lax.axis_size("space")
+    frames, rows, columns, inner = value_ref.shape
+    tokens = frames * rows * columns
+    depth, cols = weight_ref.shape
+    width = inner // heads
+    groups = ns // 2
+    half = inner // 2
+    blocks, parts, _, lane = weights.shape
+    chips = ns // 4
+    row_tokens = rows * columns
+    span = 2 * frames
+
+    p = lax.rem(t, 2)
+    column_block = lax.div(t, 2)
+    c = lax.rem(s, 2)
+    z = lax.div(s, 2)
+    level = lax.rem(z, 2)
+    chip = lax.div(z, 2)
+    mate = t + 1 - 2 * p
+    partner = s + 1 - 2 * c
+    level_mate = s + 2 - 4 * level
+
+    has_low_t, has_high_t = t >= 2, t < nt - 2
+    has_low_s, has_high_s = s > 0, s < ns - 1
+
+    def remote(source, target, send, recv, tm, space):
+        return pltpu.make_async_remote_copy(
+            src_ref=source,
+            dst_ref=target,
+            send_sem=send,
+            recv_sem=recv,
+            device_id=(tm, space),
+            device_id_type=pl.DeviceIdType.MESH,
+        )
+
+    def lanes_at(start, size):
+        return pl.ds(pl.multiple_of(start, 128), size)
+
+    def other_column(e):
+        return lax.rem(column_block + e, blocks)
+
+    def other_chip(d):
+        return lax.rem(chip + d, chips)
+
+    def column_device(e):
+        return 2 * other_column(e) + p
+
+    def chip_device(d):
+        return 4 * other_chip(d) + 2 * level + c
+
+    load_key = pltpu.make_async_copy(raw_key_ref, raw.at[0], local_sem.at[0])
+    load_key.start()
+    load_query = pltpu.make_async_copy(raw_query_ref, raw.at[1], local_sem.at[1])
+    load_query.start()
+
+    barrier = pltpu.get_barrier_semaphore()
+
+    def greet(tm, space):
+        pl.semaphore_signal(
+            barrier, inc=1, device_id=(tm, space), device_id_type=pl.DeviceIdType.MESH
+        )
+
+    greet(mate, s)
+    greet(t, partner)
+    greet(t, level_mate)
+    for e in range(1, blocks):
+        greet(column_device(e), s)
+    for d in range(1, chips):
+        greet(t, chip_device(d))
+    up, down = (c == 1) & has_high_s, (c == 0) & has_low_s
+
+    @pl.when(up)
+    def _():
+        greet(t, s + 1)
+
+    @pl.when(down)
+    def _():
+        greet(t, s - 1)
+
+    pl.semaphore_wait(barrier, blocks + chips + 1 + jnp.where(up | down, 1, 0))
+
+    own_frames = pl.ds(1 + frames * p, frames)
+    own_rows = pl.ds(1, rows)
+
+    def group_lanes(b):
+        return pl.ds(b * depth, depth)
+
+    def value_swap(b):
+        source = value_ref.at[:, :, :, lanes_at((2 * b + 1 - p) * depth, depth)]
+        target = region.at[1, own_frames, own_rows, :, group_lanes(b)]
+        return remote(source, target, swap_send.at[1, b], swap_recv.at[1, b], mate, s)
+
+    def key_swap(b):
+        source = normed.at[0, 1 - p, :, :, :, group_lanes(b)]
+        target = region.at[0, own_frames, own_rows, :, group_lanes(b)]
+        return remote(source, target, swap_send.at[0, b], swap_recv.at[0, b], mate, s)
+
+    def query_swap(b):
+        source = normed.at[1, 1 - p, :, :, :, group_lanes(b)]
+        target = query_ref.at[pl.ds(frames * p, frames), :, :, group_lanes(b)]
+        return remote(source, target, swap_send.at[2, b], swap_recv.at[2, b], mate, s)
+
+    def own_value(b):
+        return pltpu.make_async_copy(
+            value_ref.at[:, :, :, lanes_at((2 * b + p) * depth, depth)],
+            region.at[1, own_frames, own_rows, :, group_lanes(b)],
+            value_sem.at[b],
+        )
+
+    def own_weight(q):
+        return weight_ref.at[:, pl.ds(q * lane, lane)]
+
+    def own_weight_at(q):
+        return weight_ref.at[:, lanes_at(q * lane, lane)]
+
+    def weight_block(block, chip_index, core, q):
+        start = (2 * chip_index + core) * depth
+        return weights.at[block, q, pl.ds(pl.multiple_of(start, depth), depth)]
+
+    def arrival(chip_index, core):
+        return 2 * chip_index + core
+
+    def keep_weight(q):
+        return pltpu.make_async_copy(
+            own_weight_at(q), weight_block(column_block, chip, c, q), own_sem.at[q]
+        )
+
+    def far_weight(d, q):
+        return remote(
+            own_weight_at(q), weight_block(column_block, chip, c, q),
+            near_send.at[d - 1, q], weight_recv.at[column_block, arrival(chip, c), q],
+            t, chip_device(d),
+        )
+
+    def cross_weight(e, d, q):
+        block = weight_block(column_block, other_chip(d), c, q)
+        source = own_weight_at(q) if d == 0 else block
+        return remote(
+            source, block, cross_send.at[e - 1, d, q],
+            weight_recv.at[column_block, arrival(other_chip(d), c), q],
+            column_device(e), s,
+        )
+
+    def pair_weight(e, d, q):
+        block = weight_block(other_column(e), other_chip(d), c, q)
+        source = own_weight_at(q) if e == 0 and d == 0 else block
+        return remote(
+            source, block, pair_send.at[e, d, q],
+            weight_recv.at[other_column(e), arrival(other_chip(d), c), q],
+            t, partner,
+        )
+
+    def weight_here(e, d, core, q):
+        block = weight_block(other_column(e), other_chip(d), core, q)
+        remote(
+            block, block, pair_send.at[e, d, q],
+            weight_recv.at[other_column(e), arrival(other_chip(d), core), q], t, partner,
+        ).wait_recv()
+
+    def send_far(q):
+        for d in range(1, chips):
+            far_weight(d, q).start()
+
+    def send_cross(q):
+        for e in range(1, blocks):
+            cross_weight(e, 0, q).start()
+        pair_weight(0, 0, q).start()
+
+    def relay_far(q):
+        for d in range(1, chips):
+            weight_here(0, d, c, q)
+            for e in range(1, blocks):
+                cross_weight(e, d, q).start()
+            pair_weight(0, d, q).start()
+
+    def relay_cross(q, far):
+        for e in range(1, blocks):
+            for d in range(1, chips) if far else (0,):
+                weight_here(e, d, c, q)
+                pair_weight(e, d, q).start()
+
+    value_swap(0).start()
+    for b in range(groups):
+        own_value(b).start()
+    send_far(0)
+    send_cross(0)
+    for q in range(parts):
+        keep_weight(q).start()
+    own_hidden = pltpu.make_async_copy(hidden_in_ref, hidden_ref, local_sem.at[2])
+    own_hidden.start()
+
+    step = 16 if columns % 16 == 0 else columns
+
+    def normalize(index, gain_ref):
+        for frame in range(frames):
+            for row in range(rows):
+                for column in range(0, columns, step):
+                    at = slice(column, column + step)
+                    result = normalized(raw[index, frame, row, at], gain_ref[...])
+                    for b in range(groups):
+                        for core in range(2):
+                            start = (2 * b + core) * depth
+                            normed[index, core, frame, row, at, b * depth:(b + 1) * depth] = (
+                                result[:, start:start + depth]
+                            )
+
+    load_key.wait()
+    with jax.named_scope("normalize_key"):
+        normalize(0, key_gain_ref)
+    key_swap(0).start()
+    own_key = pltpu.make_async_copy(
+        normed.at[0, p], region.at[0, own_frames, own_rows], local_sem.at[3]
+    )
+    own_key.start()
+    load_query.wait()
+    with jax.named_scope("normalize_query"):
+        normalize(1, query_gain_ref)
+    query_swap(0).start()
+    own_query = pltpu.make_async_copy(
+        normed.at[1, p], query_ref.at[pl.ds(frames * p, frames)], local_sem.at[4]
+    )
+    own_query.start()
+    for b in range(1, groups):
+        value_swap(b).start()
+        key_swap(b).start()
+        query_swap(b).start()
+
+    def clear_frame(frame):
+        def run():
+            for part in range(2):
+                for row in range(rows + 2):
+                    region[part, frame, row] = jnp.zeros((columns, half), jnp.bfloat16)
+        return run
+
+    def clear_row(row):
+        def run():
+            for part in range(2):
+                for frame in range(span + 2):
+                    region[part, frame, row] = jnp.zeros((columns, half), jnp.bfloat16)
+        return run
+
+    pl.when(jnp.logical_not(has_low_t))(clear_frame(0))
+    pl.when(jnp.logical_not(has_high_t))(clear_frame(span + 1))
+    pl.when(jnp.logical_not(has_low_s))(clear_row(0))
+    pl.when(jnp.logical_not(has_high_s))(clear_row(rows + 1))
+
+    frame_k, row_k, tile_k = key_place_ref[0:1], key_place_ref[1:2], key_place_ref[2:3]
+    inside = (row_k >= -s * rows) & (row_k < (ns - s) * rows)
+    row_gap = jnp.abs(query_place_ref[:, 0:1] - row_k) + jnp.where(inside, 0, 9)
+    tile_gap = jnp.abs(query_place_ref[:, 1:2] - tile_k)
+    low_gap = jnp.where(has_low_t, 0, 9) * (frame_k < 0).astype(jnp.int32)
+    high_gap = jnp.where(has_high_t, 0, 9) * (frame_k > 0).astype(jnp.int32)
+    for kind, edge in enumerate((jnp.zeros_like(low_gap), low_gap, high_gap)):
+        frame_gap = jnp.abs(frame_k) + edge
+        for i, (reach_t, reach_r, reach_c) in enumerate(REACHES):
+            allowed = (frame_gap <= reach_t) & (row_gap <= reach_r) & (tile_gap <= reach_c)
+            mask_ref[kind, i] = jnp.where(allowed, 0.0, -1e30)
+
+    pair_frames = pl.ds(1, span)
+
+    def row_up(b):
+        return remote(
+            region.at[:, pair_frames, rows, :, group_lanes(b)],
+            region.at[:, pair_frames, 0, :, group_lanes(b)],
+            side_send.at[0, b], side_recv.at[0, b], t, s + 1,
+        )
+
+    def row_down(b):
+        return remote(
+            region.at[:, pair_frames, 1, :, group_lanes(b)],
+            region.at[:, pair_frames, rows + 1, :, group_lanes(b)],
+            side_send.at[1, b], side_recv.at[1, b], t, s - 1,
+        )
+
+    def frame_up(b):
+        return remote(
+            region.at[:, span, own_rows, :, group_lanes(b)],
+            region.at[:, 0, own_rows, :, group_lanes(b)],
+            side_send.at[2, b], side_recv.at[2, b], t + 2, s,
+        )
+
+    def frame_down(b):
+        return remote(
+            region.at[:, 1, own_rows, :, group_lanes(b)],
+            region.at[:, span + 1, own_rows, :, group_lanes(b)],
+            side_send.at[3, b], side_recv.at[3, b], t - 2, s,
+        )
+
+    def sides(b):
+        return (
+            (frame_up(b), has_high_t, has_low_t),
+            (frame_down(b), has_low_t, has_high_t),
+            (row_up(b), has_high_s, has_low_s),
+            (row_down(b), has_low_s, has_high_s),
+        )
+
+    def corners(b):
+        result = []
+        for i, (frame, has_frame) in enumerate(((0, has_low_t), (span + 1, has_high_t))):
+            for j, (row, landing, space, sends, receives) in enumerate((
+                (rows, 0, s + 1, has_high_s, has_low_s),
+                (1, rows + 1, s - 1, has_low_s, has_high_s),
+            )):
+                copy = remote(
+                    region.at[:, frame, row, :, group_lanes(b)],
+                    region.at[:, frame, landing, :, group_lanes(b)],
+                    corner_send.at[2 * i + j, b], corner_recv.at[2 * i + j, b], t, space,
+                )
+                result.append((copy, has_frame & sends, has_frame & receives))
+        return result
+
+    def feature_lanes(index, core):
+        return lanes_at((2 * index + core) * depth, depth)
+
+    def to_level_mate(j):
+        at = (slice(None), feature_lanes(j, p))
+        return remote(
+            mixed.at[(2,) + at], mixed.at[(level,) + at],
+            level_send.at[j], level_recv.at[j], t, level_mate,
+        )
+
+    def from_level_mate(j):
+        at = (1 - level, slice(None), feature_lanes(j, p))
+        return remote(mixed.at[at], mixed.at[at], level_send.at[j], level_recv.at[j], t, level_mate)
+
+    def to_mate(which, j):
+        at = (which, slice(None), feature_lanes(j, p))
+        return remote(
+            mixed.at[at], mixed.at[at], mixed_send.at[which, j], mixed_recv.at[which, j], mate, s
+        )
+
+    def from_mate(which, j):
+        at = (which, slice(None), feature_lanes(j, 1 - p))
+        remote(
+            mixed.at[at], mixed.at[at], mixed_send.at[which, j], mixed_recv.at[which, j], mate, s
+        ).wait_recv()
+
+    def attend(b):
+        in_level = level == b % 2
+        place = jnp.where(in_level, level, 2)
+        index = b // 2
+        group = depth // width
+
+        def one_head(i, carry):
+            h = (2 * b + p) * group + i
+            lanes = lanes_at(b * depth + i * width, width)
+            reach = time_ref[h] * 6 + rows_ref[h] * 3 + cols_ref[h]
+            target = lanes_at((2 * index + p) * depth + i * width, width)
+            scores, values = [], []
+            for frame in range(span):
+                query = query_ref[frame, :, :, lanes].reshape(row_tokens, width)
+                near = slice(frame, frame + 3)
+                key = region[0, near, :, :, lanes].reshape(-1, width)
+                values.append(region[1, near, :, :, lanes].reshape(-1, width))
+                scores.append(lax.dot_general(
+                    query, key, (((1,), (1,)), ((), ())), preferred_element_type=jnp.float32
+                ))
+            results = []
+            for frame in range(span):
+                kind = 1 if frame == 0 else 2 if frame == span - 1 else 0
+                masked = scores[frame] * width ** (-0.5) + mask_ref[kind, reach]
+                part = jnp.exp(masked - jnp.max(masked, axis=1, keepdims=True))
+                sums = jnp.sum(part, axis=1, keepdims=True)
+                result = jnp.dot(
+                    part.astype(jnp.bfloat16), values[frame], preferred_element_type=jnp.float32
+                )
+                results.append((result / sums).astype(jnp.bfloat16))
+            mixed[place, :, target] = jnp.concatenate(results, axis=0)
+            return carry
+
+        lax.fori_loop(0, group, one_head, 0)
+
+    def send_mixed(b):
+        in_level = level == b % 2
+        index = b // 2
+        pl.when(in_level)(to_mate(level, index).start)
+        pl.when(jnp.logical_not(in_level))(to_level_mate(index).start)
+
+    def relay_mixed(b):
+        @pl.when(level == b % 2)
+        def _():
+            from_level_mate(b // 2).wait_recv()
+            to_mate(1 - level, b // 2).start()
+
+    def arrive(i):
+        with jax.named_scope(f"wait_swap{i}"):
+            value_swap(i).wait_recv()
+            key_swap(i).wait_recv()
+            own_value(i).wait()
+            if i == 0:
+                own_key.wait()
+        with jax.named_scope(f"send_sides{i}"):
+            for copy, sends, _ in sides(i):
+                pl.when(sends)(copy.start)
+
+    def turn(i):
+        with jax.named_scope(f"wait_frames{i}"):
+            for copy, _, receives in sides(i)[:2]:
+                pl.when(receives)(copy.wait_recv)
+        for copy, sends, _ in corners(i):
+            pl.when(sends)(copy.start)
+
+    def ready(b):
+        with jax.named_scope(f"wait_query{b}"):
+            query_swap(b).wait_recv()
+            if b == 0:
+                own_query.wait()
+        with jax.named_scope(f"wait_rows{b}"):
+            for copy, _, receives in sides(b)[2:]:
+                pl.when(receives)(copy.wait_recv)
+        with jax.named_scope(f"wait_corners{b}"):
+            for copy, _, receives in corners(b):
+                pl.when(receives)(copy.wait_recv)
+
+    early = min(2, parts)
+    for i in range(groups + 1):
+        if i < groups:
+            arrive(i)
+        if i > 0:
+            ready(i - 1)
+            with jax.named_scope(f"attend{i - 1}"):
+                attend(i - 1)
+        if i < groups:
+            turn(i)
+        if i > 0:
+            send_mixed(i - 1)
+        if i == 1 and parts > 1:
+            send_far(1)
+        if i == groups - 1 and parts > 2:
+            send_far(2)
+        if i < groups:
+            if i + 1 < min(groups, parts):
+                send_cross(i + 1)
+        else:
+            if parts > 3:
+                send_far(3)
+            for q in range(early):
+                relay_far(q)
+            for q in range(groups, parts):
+                send_cross(q)
+        if i > 1:
+            with jax.named_scope(f"relay_mixed{i}"):
+                relay_mixed(i - 2)
+        if i > 1 and i - 2 < parts:
+            with jax.named_scope(f"relay_cross{i}"):
+                relay_cross(i - 2, False)
+    with jax.named_scope("relay_mixed_last"):
+        relay_mixed(groups - 1)
+
+    def each_part(low, high, run):
+        def body(q, carry):
+            run(q)
+            return carry
+
+        lax.fori_loop(low, high, body, 0)
+
+    def next_far(q):
+        if q < parts:
+            with jax.named_scope(f"relay_far{q}"):
+                relay_far(q)
+            if q + 2 < parts:
+                send_far(q + 2)
+
+    next_far(early)
+    with jax.named_scope("from_mate"):
+        for which in range(2):
+            for j in range(groups // 2):
+                from_mate(which, j)
+
+    def multiply(e, q):
+        block = other_column(e)
+        for d in range(chips):
+            weight_here(e, d, 1 - c, q)
+        left = mixed[0:2].reshape(4 * tokens, half)
+        product = jnp.dot(left, weights[block, q], preferred_element_type=jnp.float32)
+        total[block, q] = product.reshape(2, 2 * tokens, lane)
+        partial_out[block, q] = total[block, q, 1 - level].astype(jnp.bfloat16)
+        part_copy(block, q).start()
+
+    def part_copy(block, q):
+        return remote(
+            partial_out.at[block, q], partial_in.at[block, q],
+            part_send.at[block, q], part_recv.at[block, q], t, level_mate,
+        )
+
+    def back(block, q):
+        return remote(
+            outgoing.at[block, q], incoming.at[block, q],
+            back_send.at[block, q], back_recv.at[block, q], mate, s,
+        )
+
+    def token_rows(side):
+        return pl.ds(pl.multiple_of(side * tokens, tokens), tokens)
+
+    def finish(column, branch):
+        lanes = lanes_at(column, lane)
+        out_ref[:, lanes] = (
+            hidden_ref[:, lanes].astype(jnp.float32) + gate_ref[:, lanes] * branch
+        ).astype(jnp.bfloat16)
+
+    def reduce_part(q):
+        for e in range(blocks):
+            block = other_column(e)
+            part_copy(block, q).wait_recv()
+            theirs = token_rows(1 - p)
+            outgoing[block, q] = (
+                total[block, q, level, theirs] + partial_in[block, q, theirs].astype(jnp.float32)
+            ).astype(jnp.bfloat16)
+            back(block, q).start()
+            ours = token_rows(p)
+            branch = total[block, q, level, ours] + partial_in[block, q, ours].astype(jnp.float32)
+            finish((2 * block + p) * cols + q * lane, branch)
+
+    own_hidden.wait()
+    reduced = 0
+    for q in range(parts):
+        if q >= groups - 1:
+            relay_cross(q, False)
+        keep_weight(q).wait()
+        with jax.named_scope(f"multiply{q}own"):
+            multiply(0, q)
+        if blocks > 1:
+            with jax.named_scope(f"main_cross{q}"):
+                relay_cross(q, True)
+            with jax.named_scope(f"multiply{q}other"):
+                for e in range(1, blocks):
+                    multiply(e, q)
+        if q >= 1:
+            next_far(early + q)
+        with jax.named_scope(f"reduce{q}"):
+            while reduced < q - 1:
+                reduce_part(reduced)
+                reduced += 1
+    with jax.named_scope("reduce_last"):
+        each_part(reduced, parts, reduce_part)
+
+    def finish_others(q):
+        for block in range(blocks):
+            back(block, q).wait_recv()
+            finish((2 * block + 1 - p) * cols + q * lane, incoming[block, q].astype(jnp.float32))
+
+    with jax.named_scope("finish_others"):
+        each_part(0, parts, finish_others)
+
+    for b in range(groups):
+        value_swap(b).wait_send()
+        key_swap(b).wait_send()
+        query_swap(b).wait_send()
+        for copy, sends, _ in sides(b) + tuple(corners(b)):
+            pl.when(sends)(copy.wait_send)
+    for j in range(groups // 2):
+        to_level_mate(j).wait_send()
+        for which in range(2):
+            to_mate(which, j).wait_send()
+
+    def sent(q):
+        for d in range(1, chips):
+            far_weight(d, q).wait_send()
+        for e in range(blocks):
+            for d in range(chips):
+                pair_weight(e, d, q).wait_send()
+                if e > 0:
+                    cross_weight(e, d, q).wait_send()
+        for block in range(blocks):
+            part_copy(block, q).wait_send()
+            back(block, q).wait_send()
+
+    each_part(0, parts, sent)
+
+
+def pair_shards(
+    hidden_in,
+    queries,
+    keys,
+    values,
+    query_gain,
+    key_gain,
+    reach_time,
+    reach_rows,
+    reach_cols,
+    out_weight,
+    gate,
+):
+    frames, rows, columns, inner = queries.shape
+    width = hidden_in.shape[3]
+    heads = reach_time.shape[0]
+    tokens = frames * rows * columns
+    nt, ns = lax.axis_size("tm"), lax.axis_size("space")
+    depth, cols = out_weight.shape
+    lane = 256 if cols % 256 == 0 else 128
+    parts = cols // lane
+    blocks, chips, groups = nt // 2, ns // 4, ns // 2
+    half = inner // 2
+    pair_tokens = 2 * tokens
+    vmem = pl.BlockSpec(memory_space=pltpu.VMEM)
+    hbm = pl.BlockSpec(memory_space=pl.ANY)
+    dma = pltpu.SemaphoreType.DMA
+    _, query_row, query_tile = places(1, rows, columns, 0)
+    key_place = np.stack([axis.reshape(-1) for axis in np.meshgrid(
+        np.arange(-1, 2), np.arange(-1, rows + 1), np.arange(columns) // TW, indexing="ij"
+    )]).astype(np.int32)
+    output = pl.pallas_call(
+        functools.partial(pair_kernel, heads),
+        out_shape=jax.ShapeDtypeStruct((tokens, width), jnp.bfloat16),
+        in_specs=[pl.BlockSpec(memory_space=pltpu.SMEM)] * 3 + [vmem] * 5 + [hbm] * 5,
+        out_specs=vmem,
+        scratch_shapes=[
+            pltpu.VMEM((2, frames, rows, columns, inner), jnp.bfloat16),
+            pltpu.VMEM((2, 2, frames, rows, columns, half), jnp.bfloat16),
+            pltpu.VMEM((2, 2 * frames + 2, rows + 2, columns, half), jnp.bfloat16),
+            pltpu.VMEM((2 * frames, rows, columns, half), jnp.bfloat16),
+            pltpu.VMEM((3, len(REACHES), rows * columns, 3 * (rows + 2) * columns), jnp.float32),
+            pltpu.VMEM((3, pair_tokens, half), jnp.bfloat16),
+            pltpu.VMEM((blocks, parts, half, lane), jnp.bfloat16),
+            pltpu.VMEM((blocks, parts, 2, pair_tokens, lane), jnp.float32),
+            pltpu.VMEM((blocks, parts, pair_tokens, lane), jnp.bfloat16),
+            pltpu.VMEM((blocks, parts, pair_tokens, lane), jnp.bfloat16),
+            pltpu.VMEM((blocks, parts, tokens, lane), jnp.bfloat16),
+            pltpu.VMEM((blocks, parts, tokens, lane), jnp.bfloat16),
+            pltpu.VMEM((tokens, width), jnp.bfloat16),
+            dma((5,)),
+            dma((groups,)),
+            dma((parts,)),
+            dma((3, groups)),
+            dma((3, groups)),
+            dma((4, groups)),
+            dma((4, groups)),
+            dma((4, groups)),
+            dma((4, groups)),
+            dma((max(chips - 1, 1), parts)),
+            dma((max(blocks - 1, 1), chips, parts)),
+            dma((blocks, chips, parts)),
+            dma((blocks, 2 * chips, parts)),
+            dma((groups // 2,)),
+            dma((groups // 2,)),
+            dma((2, groups // 2)),
+            dma((2, groups // 2)),
+            dma((blocks, parts)),
+            dma((blocks, parts)),
+            dma((blocks, parts)),
+            dma((blocks, parts)),
+        ],
+        compiler_params=pltpu.CompilerParams(
+            collective_id=0, has_side_effects=True, vmem_limit_bytes=60 * 1024 * 1024
+        ),
+    )(
+        reach_time,
+        reach_rows,
+        reach_cols,
+        query_gain.reshape(1, inner),
+        key_gain.reshape(1, inner),
+        np.stack([query_row, query_tile]).T,
+        key_place,
+        gate.reshape(1, width),
+        queries,
+        keys,
+        values,
+        out_weight,
+        hidden_in.reshape(tokens, width),
+    )
+    return output.reshape(frames, rows, columns, width)
+
+
+def shards(hidden_in, queries, keys, values, *others):
+    out_weight, reach_time = others[-2], others[2]
+    width = queries.shape[3] // reach_time.shape[0]
+    nt, ns = lax.axis_size("tm"), lax.axis_size("space")
+    whole_heads = out_weight.shape[0] % width == 0
+    form = pair_shards if whole_heads and nt % 2 == 0 and ns % 4 == 0 else ring_shards
+    return form(hidden_in, queries, keys, values, *others)
+
+
 def solution(mesh):
     in_specs = (
         P("tm", "space", None, None),

time: 171 us -> 131 us (0.77); the launches traced: 169 us -> 131 us
  Pallas kernels: 166 us -> 128 us
    pallas_call x1, Pallas kernels: 166 us -> 128 us  [pair_shards(): pl.pallas_call(functools.partial(pair_kernel, heads), out_shape=jax.Shape...]
where the time goes in v1:
time: 131 us
  Pallas kernels  128 us (98%)
  local copies, waits for them, and re-layouts  2.46 us (2%)
    pallas_call x1, Pallas kernels, pair_shards(): pl.pallas_call(functools.partial(pair_kernel, heads), out_shape=jax.Shape...  128 us

profile of v1, /device:TPU:0, one launch (start us, length us, event | category | flops | bytes accessed | tf_op | source)
XLA Modules:
  0.0 130.8 jit_solution(5826527723821756141)
XLA Ops:
  0.0 128.4 %shard_map.127 = bf16[128,5120]{1,0:T(8,128)(2,1)} custom-call(s32[40]{0:T(128)} %time_ref.1, s32[40]{0:T(128)} %rows_ref.1, s32[40]{0:T(128)} %cols_ref.1, f32[1,5120]{1,0:T(1,128)} %bitcast.7, f32[1,5120]{1,0:T(1,128)} %bitcast.8, s32[64,2]{1,0:T(8,128)} %constant.4.clone.query_place_ref, s32[3,384]{1,0:T(4,128)} %constant.5.clone.key_place_ref, ...), custom_call_target="tpu_custom_call" | custom-call | tf_op jit(solution)/shard_map/pallas_call | solution.py:1138
  128.4 2.5 %copy.15 = bf16[2,2,32,5120]{3,2,1,0:T(8,128)(2,1)} copy(bf16[2,2,32,5120]{3,2,1,0:T(8,128)(2,1)} %bitcast.5) | data formatting | bytes 2621440

commit v2 on v1

--- a/solution.py
+++ b/solution.py
@@ -509,6 +509,7 @@
     outgoing,
     incoming,
     hidden_ref,
+    staged,
     local_sem,
     value_sem,
     own_sem,
@@ -518,6 +519,7 @@
     side_recv,
     corner_send,
     corner_recv,
+    stage_recv,
     near_send,
     cross_send,
     pair_send,
@@ -584,6 +586,17 @@
     def chip_device(d):
         return 4 * other_chip(d) + 2 * level + c
 
+    levels = 2 * chips
+    middle = levels // 2
+
+    def comes_late(d):
+        rises = other_chip(d) < chip
+        return (rises & (z <= middle)) | (jnp.logical_not(rises) & (z + 1 >= middle))
+
+    starts = {True: z + 2 < levels, False: z >= 2}
+    passes = {True: (z >= 1) & (z + 1 < levels), False: (z + 1 < levels) & (z >= 1)}
+    inner = {True: z < middle, False: z >= middle}
+
     load_key = pltpu.make_async_copy(raw_key_ref, raw.at[0], local_sem.at[0])
     load_key.start()
     load_query = pltpu.make_async_copy(raw_query_ref, raw.at[1], local_sem.at[1])
@@ -601,8 +614,9 @@
     greet(t, level_mate)
     for e in range(1, blocks):
         greet(column_device(e), s)
-    for d in range(1, chips):
-        greet(t, chip_device(d))
+    across = s - 2 + 4 * level
+    has_across = (across >= 0) & (across < ns)
+    pl.when(has_across)(functools.partial(greet, t, across))
     up, down = (c == 1) & has_high_s, (c == 0) & has_low_s
 
     @pl.when(up)
@@ -613,7 +627,9 @@
     def _():
         greet(t, s - 1)
 
-    pl.semaphore_wait(barrier, blocks + chips + 1 + jnp.where(up | down, 1, 0))
+    pl.semaphore_wait(
+        barrier, blocks + 2 + has_across.astype(jnp.int32) + (up | down).astype(jnp.int32)
+    )
 
     own_frames = pl.ds(1 + frames * p, frames)
     own_rows = pl.ds(1, rows)
@@ -661,11 +677,20 @@
             own_weight_at(q), weight_block(column_block, chip, c, q), own_sem.at[q]
         )
 
-    def far_weight(d, q):
+    def first_hop(rising, q):
         return remote(
-            own_weight_at(q), weight_block(column_block, chip, c, q),
-            near_send.at[d - 1, q], weight_recv.at[column_block, arrival(chip, c), q],
-            t, chip_device(d),
+            own_weight_at(q), staged.at[int(rising), q],
+            near_send.at[0, int(rising), q], stage_recv.at[int(rising), q],
+            t, s + 2 if rising else s - 2,
+        )
+
+    def second_hop(rising, q):
+        origin = lax.div(z + levels - 1 if rising else z + levels + 1, 2) - chips
+        return remote(
+            staged.at[int(rising), q], weight_block(column_block, origin, c, q),
+            near_send.at[1, int(rising), q],
+            weight_recv.at[column_block, arrival(origin, c), q],
+            t, s + 2 if rising else s - 2,
         )
 
     def cross_weight(e, d, q):
@@ -693,21 +718,32 @@
             weight_recv.at[other_column(e), arrival(other_chip(d), core), q], t, partner,
         ).wait_recv()
 
-    def send_far(q):
-        for d in range(1, chips):
-            far_weight(d, q).start()
+    at_end = (z == 0) | (z == levels - 1)
+
+    def send_far(q, ends, which=True):
+        for rising in (True, False):
+            pl.when(starts[rising] & (at_end == ends) & which)(first_hop(rising, q).start)
+
+    def forward(q, inward, which=True):
+        for rising in (True, False):
+            @pl.when(passes[rising] & (inner[rising] == inward) & which)
+            def _(rising=rising):
+                first_hop(rising, q).wait_recv()
+                second_hop(rising, q).start()
 
     def send_cross(q):
         for e in range(1, blocks):
             cross_weight(e, 0, q).start()
         pair_weight(0, 0, q).start()
 
-    def relay_far(q):
+    def relay_far(q, late):
         for d in range(1, chips):
-            weight_here(0, d, c, q)
-            for e in range(1, blocks):
-                cross_weight(e, d, q).start()
-            pair_weight(0, d, q).start()
+            @pl.when(comes_late(d) if late else jnp.logical_not(comes_late(d)))
+            def _(d=d):
+                weight_here(0, d, c, q)
+                for e in range(1, blocks):
+                    cross_weight(e, d, q).start()
+                pair_weight(0, d, q).start()
 
     def relay_cross(q, far):
         for e in range(1, blocks):
@@ -718,7 +754,8 @@
     value_swap(0).start()
     for b in range(groups):
         own_value(b).start()
-    send_far(0)
+    send_far(0, True)
+    send_far(0, False)
     send_cross(0)
     for q in range(parts):
         keep_weight(q).start()
@@ -907,16 +944,14 @@
         lax.fori_loop(0, group, one_head, 0)
 
     def send_mixed(b):
-        in_level = level == b % 2
-        index = b // 2
-        pl.when(in_level)(to_mate(level, index).start)
-        pl.when(jnp.logical_not(in_level))(to_level_mate(index).start)
+        pl.when(level != b % 2)(to_level_mate(b // 2).start)
 
     def relay_mixed(b):
         @pl.when(level == b % 2)
         def _():
             from_level_mate(b // 2).wait_recv()
             to_mate(1 - level, b // 2).start()
+            to_mate(level, b // 2).start()
 
     def arrive(i):
         with jax.named_scope(f"wait_swap{i}"):
@@ -949,6 +984,26 @@
                 pl.when(receives)(copy.wait_recv)
 
     early = min(2, parts)
+    actions = {
+        "end": lambda q: send_far(q, True),
+        "end0": lambda q: send_far(q, True, level == 0),
+        "end1": lambda q: send_far(q, True, level == 1),
+        "out0": lambda q: forward(q, False, level == 0),
+        "out1": lambda q: forward(q, False, level == 1),
+        "mid": lambda q: send_far(q, False),
+        "late": lambda q: relay_far(q, True),
+        "cross": send_cross,
+        "out": lambda q: forward(q, False),
+        "in": lambda q: forward(q, True),
+        "early": lambda q: relay_far(q, False),
+    }
+    plan = {i: [] for i in range(groups + 1)}
+    plan[0] += [("mid", 1), ("end", 1), ("cross", 1), ("out", 0)]
+    plan[1] += [("mid", 2), ("end0", 2), ("cross", 2), ("out0", 1)]
+    plan[2] += [("mid", 3), ("end1", 2), ("cross", 3), ("out1", 1)]
+    plan[3] += [("in", 0), ("mid", 4), ("end0", 3), ("out0", 2), ("cross", 4), ("early", 0), ("early", 1)]
+    plan[groups] += [("in", 1), ("end1", 3), ("end", 4), ("out1", 2), ("out", 3), ("late", 0)]
+    plan[groups] += [("cross", q) for q in range(5, parts)]
     for i in range(groups + 1):
         if i < groups:
             arrive(i)
@@ -960,20 +1015,9 @@
             turn(i)
         if i > 0:
             send_mixed(i - 1)
-        if i == 1 and parts > 1:
-            send_far(1)
-        if i == groups - 1 and parts > 2:
-            send_far(2)
-        if i < groups:
-            if i + 1 < min(groups, parts):
-                send_cross(i + 1)
-        else:
-            if parts > 3:
-                send_far(3)
-            for q in range(early):
-                relay_far(q)
-            for q in range(groups, parts):
-                send_cross(q)
+        for kind, q in plan[i]:
+            if q < parts:
+                actions[kind](q)
         if i > 1:
             with jax.named_scope(f"relay_mixed{i}"):
                 relay_mixed(i - 2)
@@ -993,25 +1037,23 @@
     def next_far(q):
         if q < parts:
             with jax.named_scope(f"relay_far{q}"):
-                relay_far(q)
-            if q + 2 < parts:
-                send_far(q + 2)
-
-    next_far(early)
-    with jax.named_scope("from_mate"):
-        for which in range(2):
-            for j in range(groups // 2):
-                from_mate(which, j)
-
-    def multiply(e, q):
+                relay_far(q, True)
+
+    def multiply_theirs(e, q):
         block = other_column(e)
         for d in range(chips):
             weight_here(e, d, 1 - c, q)
-        left = mixed[0:2].reshape(4 * tokens, half)
-        product = jnp.dot(left, weights[block, q], preferred_element_type=jnp.float32)
-        total[block, q] = product.reshape(2, 2 * tokens, lane)
-        partial_out[block, q] = total[block, q, 1 - level].astype(jnp.bfloat16)
+        product = jnp.dot(
+            mixed[1 - level], weights[block, q], preferred_element_type=jnp.float32
+        )
+        partial_out[block, q] = product.astype(jnp.bfloat16)
         part_copy(block, q).start()
+
+    def multiply_ours(e, q):
+        block = other_column(e)
+        total[block, q] = jnp.dot(
+            mixed[level], weights[block, q], preferred_element_type=jnp.float32
+        )
 
     def part_copy(block, q):
         return remote(
@@ -1040,43 +1082,81 @@
             part_copy(block, q).wait_recv()
             theirs = token_rows(1 - p)
             outgoing[block, q] = (
-                total[block, q, level, theirs] + partial_in[block, q, theirs].astype(jnp.float32)
+                total[block, q, theirs] + partial_in[block, q, theirs].astype(jnp.float32)
             ).astype(jnp.bfloat16)
             back(block, q).start()
             ours = token_rows(p)
-            branch = total[block, q, level, ours] + partial_in[block, q, ours].astype(jnp.float32)
+            branch = total[block, q, ours] + partial_in[block, q, ours].astype(jnp.float32)
             finish((2 * block + p) * cols + q * lane, branch)
 
-    own_hidden.wait()
-    reduced = 0
-    for q in range(parts):
+    def theirs(q):
         if q >= groups - 1:
             relay_cross(q, False)
         keep_weight(q).wait()
-        with jax.named_scope(f"multiply{q}own"):
-            multiply(0, q)
+        with jax.named_scope(f"theirs{q}own"):
+            multiply_theirs(0, q)
         if blocks > 1:
             with jax.named_scope(f"main_cross{q}"):
                 relay_cross(q, True)
-            with jax.named_scope(f"multiply{q}other"):
+            with jax.named_scope(f"theirs{q}other"):
                 for e in range(1, blocks):
-                    multiply(e, q)
-        if q >= 1:
-            next_far(early + q)
-        with jax.named_scope(f"reduce{q}"):
-            while reduced < q - 1:
-                reduce_part(reduced)
-                reduced += 1
-    with jax.named_scope("reduce_last"):
-        each_part(reduced, parts, reduce_part)
+                    multiply_theirs(e, q)
+
+    def ours(q):
+        with jax.named_scope(f"ours{q}"):
+            for e in range(blocks):
+                multiply_ours(e, q)
+
+    forward(2, True)
+    relay_far(2, False)
+    forward(4, False)
+    forward(3, True)
+    relay_far(3, False)
+    next_far(1)
+    with jax.named_scope("from_mate_theirs"):
+        for j in range(groups // 2):
+            from_mate(1 - level, j)
+    theirs(0)
+    forward(4, True)
+    next_far(2)
+    theirs(1)
+    relay_far(4, False)
+    with jax.named_scope("from_mate_ours"):
+        for j in range(groups // 2):
+            from_mate(level, j)
+    ours(0)
+    own_hidden.wait()
+    next_far(3)
+    theirs(2)
+    ours(1)
+    with jax.named_scope("reduce0"):
+        reduce_part(0)
+    next_far(4)
+    theirs(3)
+    ours(2)
+    with jax.named_scope("reduce1"):
+        reduce_part(1)
+    theirs(4)
+    ours(3)
+    ours(4)
 
     def finish_others(q):
         for block in range(blocks):
             back(block, q).wait_recv()
             finish((2 * block + 1 - p) * cols + q * lane, incoming[block, q].astype(jnp.float32))
 
-    with jax.named_scope("finish_others"):
-        each_part(0, parts, finish_others)
+    with jax.named_scope("reduce2"):
+        reduce_part(2)
+    with jax.named_scope("finish01"):
+        each_part(0, 2, finish_others)
+    with jax.named_scope("reduce3"):
+        reduce_part(3)
+    with jax.named_scope("finish2"):
+        finish_others(2)
+    with jax.named_scope("reduce4"):
+        reduce_part(4)
+    with jax.named_scope("finish34"):
+        each_part(3, parts, finish_others)
 
     for b in range(groups):
         value_swap(b).wait_send()
@@ -1090,8 +1170,9 @@
             to_mate(which, j).wait_send()
 
     def sent(q):
-        for d in range(1, chips):
-            far_weight(d, q).wait_send()
+        for rising in (True, False):
+            pl.when(starts[rising])(first_hop(rising, q).wait_send)
+            pl.when(passes[rising])(second_hop(rising, q).wait_send)
         for e in range(blocks):
             for d in range(chips):
                 pair_weight(e, d, q).wait_send()
@@ -1148,12 +1229,13 @@
             pltpu.VMEM((3, len(REACHES), rows * columns, 3 * (rows + 2) * columns), jnp.float32),
             pltpu.VMEM((3, pair_tokens, half), jnp.bfloat16),
             pltpu.VMEM((blocks, parts, half, lane), jnp.bfloat16),
-            pltpu.VMEM((blocks, parts, 2, pair_tokens, lane), jnp.float32),
+            pltpu.VMEM((blocks, parts, pair_tokens, lane), jnp.float32),
             pltpu.VMEM((blocks, parts, pair_tokens, lane), jnp.bfloat16),
             pltpu.VMEM((blocks, parts, pair_tokens, lane), jnp.bfloat16),
             pltpu.VMEM((blocks, parts, tokens, lane), jnp.bfloat16),
             pltpu.VMEM((blocks, parts, tokens, lane), jnp.bfloat16),
             pltpu.VMEM((tokens, width), jnp.bfloat16),
+            pltpu.VMEM((2, parts, depth, lane), jnp.bfloat16),
             dma((5,)),
             dma((groups,)),
             dma((parts,)),
@@ -1163,7 +1245,8 @@
             dma((4, groups)),
             dma((4, groups)),
             dma((4, groups)),
-            dma((max(chips - 1, 1), parts)),
+            dma((2, parts)),
+            dma((2, 2, parts)),
             dma((max(blocks - 1, 1), chips, parts)),
             dma((blocks, chips, parts)),
             dma((blocks, 2 * chips, parts)),
@@ -1202,7 +1285,7 @@
     width = queries.shape[3] // reach_time.shape[0]
     nt, ns = lax.axis_size("tm"), lax.axis_size("space")
     whole_heads = out_weight.shape[0] % width == 0
-    form = pair_shards if whole_heads and nt % 2 == 0 and ns % 4 == 0 else ring_shards
+    form = pair_shards if whole_heads and nt % 2 == 0 and ns // 4 == 2 else ring_shards
     return form(hidden_in, queries, keys, values, *others)
 
 

time: 131 us -> 126 us (0.962)
  the two profiles are of different devices: /device:TPU:0 before, /device:TPU:11 now
where the time goes in v2:
time: 126 us
  Pallas kernels  124 us (98%)
  local copies, waits for them, and re-layouts  2.46 us (2%)
    pallas_call x1, Pallas kernels, pair_shards(): pl.pallas_call(functools.partial(pair_kernel, heads), out_shape=jax.Shape...  124 us

profile of v2, /device:TPU:11, one launch (start us, length us, event | category | flops | bytes accessed | tf_op | source)
XLA Modules:
  0.0 126.3 jit_solution(619328966496127439)
XLA Ops:
  0.0 123.8 %shard_map.127 = bf16[128,5120]{1,0:T(8,128)(2,1)} custom-call(s32[40]{0:T(128)} %time_ref.1, s32[40]{0:T(128)} %rows_ref.1, s32[40]{0:T(128)} %cols_ref.1, f32[1,5120]{1,0:T(1,128)} %bitcast.7, f32[1,5120]{1,0:T(1,128)} %bitcast.8, s32[64,2]{1,0:T(8,128)} %constant.4.clone.query_place_ref, s32[3,384]{1,0:T(4,128)} %constant.5.clone.key_place_ref, ...), custom_call_target="tpu_custom_call" | custom-call | tf_op jit(solution)/shard_map/pallas_call | solution.py:1219
  123.8 2.5 %copy.15 = bf16[2,2,32,5120]{3,2,1,0:T(8,128)(2,1)} copy(bf16[2,2,32,5120]{3,2,1,0:T(8,128)(2,1)} %bitcast.5) | data formatting | bytes 2621440

commit v3 on v2

--- a/solution.py
+++ b/solution.py
@@ -509,6 +509,7 @@
     outgoing,
     incoming,
     hidden_ref,
+    result_ref,
     staged,
     local_sem,
     value_sem,
@@ -532,6 +533,7 @@
     part_recv,
     back_send,
     back_recv,
+    out_sem,
 ):
     t = lax.axis_index("tm")
     s = lax.axis_index("space")
@@ -677,79 +679,94 @@
             own_weight_at(q), weight_block(column_block, chip, c, q), own_sem.at[q]
         )
 
-    def first_hop(rising, q):
+    def shares(q, d=1):
+        return range(2 if d > 0 and q == parts - 1 else 1)
+
+    def rows_of(q, k, d=1):
+        count = len(shares(q, d))
+        return pl.ds(k * (depth // count), depth // count)
+
+    def first_hop(rising, q, k):
+        at = rows_of(q, k)
         return remote(
-            own_weight_at(q), staged.at[int(rising), q],
-            near_send.at[0, int(rising), q], stage_recv.at[int(rising), q],
+            own_weight_at(q).at[at], staged.at[int(rising), q, at],
+            near_send.at[0, int(rising), q + k], stage_recv.at[int(rising), q + k],
             t, s + 2 if rising else s - 2,
         )
 
-    def second_hop(rising, q):
+    def second_hop(rising, q, k):
         origin = lax.div(z + levels - 1 if rising else z + levels + 1, 2) - chips
+        at = rows_of(q, k)
         return remote(
-            staged.at[int(rising), q], weight_block(column_block, origin, c, q),
-            near_send.at[1, int(rising), q],
-            weight_recv.at[column_block, arrival(origin, c), q],
+            staged.at[int(rising), q, at], weight_block(column_block, origin, c, q).at[at],
+            near_send.at[1, int(rising), q + k],
+            weight_recv.at[column_block, arrival(origin, c), q + k],
             t, s + 2 if rising else s - 2,
         )
 
-    def cross_weight(e, d, q):
-        block = weight_block(column_block, other_chip(d), c, q)
-        source = own_weight_at(q) if d == 0 else block
+    def cross_weight(e, d, q, k):
+        at = rows_of(q, k, d)
+        block = weight_block(column_block, other_chip(d), c, q).at[at]
+        source = own_weight_at(q).at[at] if d == 0 else block
         return remote(
-            source, block, cross_send.at[e - 1, d, q],
-            weight_recv.at[column_block, arrival(other_chip(d), c), q],
+            source, block, cross_send.at[e - 1, d, q + k],
+            weight_recv.at[column_block, arrival(other_chip(d), c), q + k],
             column_device(e), s,
         )
 
-    def pair_weight(e, d, q):
-        block = weight_block(other_column(e), other_chip(d), c, q)
-        source = own_weight_at(q) if e == 0 and d == 0 else block
+    def pair_weight(e, d, q, k):
+        at = rows_of(q, k, d)
+        block = weight_block(other_column(e), other_chip(d), c, q).at[at]
+        source = own_weight_at(q).at[at] if e == 0 and d == 0 else block
         return remote(
-            source, block, pair_send.at[e, d, q],
-            weight_recv.at[other_column(e), arrival(other_chip(d), c), q],
+            source, block, pair_send.at[e, d, q + k],
+            weight_recv.at[other_column(e), arrival(other_chip(d), c), q + k],
             t, partner,
         )
 
-    def weight_here(e, d, core, q):
-        block = weight_block(other_column(e), other_chip(d), core, q)
+    def weight_here(e, d, core, q, k):
+        block = weight_block(other_column(e), other_chip(d), core, q).at[rows_of(q, k, d)]
         remote(
-            block, block, pair_send.at[e, d, q],
-            weight_recv.at[other_column(e), arrival(other_chip(d), core), q], t, partner,
+            block, block, pair_send.at[e, d, q + k],
+            weight_recv.at[other_column(e), arrival(other_chip(d), core), q + k], t, partner,
         ).wait_recv()
 
     at_end = (z == 0) | (z == levels - 1)
 
     def send_far(q, ends, which=True):
         for rising in (True, False):
-            pl.when(starts[rising] & (at_end == ends) & which)(first_hop(rising, q).start)
+            for k in shares(q):
+                pl.when(starts[rising] & (at_end == ends) & which)(first_hop(rising, q, k).start)
 
     def forward(q, inward, which=True):
         for rising in (True, False):
             @pl.when(passes[rising] & (inner[rising] == inward) & which)
             def _(rising=rising):
-                first_hop(rising, q).wait_recv()
-                second_hop(rising, q).start()
+                for k in shares(q):
+                    first_hop(rising, q, k).wait_recv()
+                    second_hop(rising, q, k).start()
 
     def send_cross(q):
         for e in range(1, blocks):
-            cross_weight(e, 0, q).start()
-        pair_weight(0, 0, q).start()
+            cross_weight(e, 0, q, 0).start()
+        pair_weight(0, 0, q, 0).start()
 
     def relay_far(q, late):
         for d in range(1, chips):
             @pl.when(comes_late(d) if late else jnp.logical_not(comes_late(d)))
             def _(d=d):
-                weight_here(0, d, c, q)
-                for e in range(1, blocks):
-                    cross_weight(e, d, q).start()
-                pair_weight(0, d, q).start()
+                for k in shares(q):
+                    weight_here(0, d, c, q, k)
+                    for e in range(1, blocks):
+                        cross_weight(e, d, q, k).start()
+                    pair_weight(0, d, q, k).start()
 
     def relay_cross(q, far):
         for e in range(1, blocks):
             for d in range(1, chips) if far else (0,):
-                weight_here(e, d, c, q)
-                pair_weight(e, d, q).start()
+                for k in shares(q, d):
+                    weight_here(e, d, c, q, k)
+                    pair_weight(e, d, q, k).start()
 
     value_swap(0).start()
     for b in range(groups):
@@ -1001,8 +1018,8 @@
     plan[0] += [("mid", 1), ("end", 1), ("cross", 1), ("out", 0)]
     plan[1] += [("mid", 2), ("end0", 2), ("cross", 2), ("out0", 1)]
     plan[2] += [("mid", 3), ("end1", 2), ("cross", 3), ("out1", 1)]
-    plan[3] += [("in", 0), ("mid", 4), ("end0", 3), ("out0", 2), ("cross", 4), ("early", 0), ("early", 1)]
-    plan[groups] += [("in", 1), ("end1", 3), ("end", 4), ("out1", 2), ("out", 3), ("late", 0)]
+    plan[3] += [("in", 0), ("end0", 3), ("out0", 2), ("cross", 4), ("early", 0), ("early", 1)]
+    plan[groups] += [("mid", 4), ("in", 1), ("end1", 3), ("end", 4), ("out1", 2), ("out", 3), ("late", 0)]
     plan[groups] += [("cross", q) for q in range(5, parts)]
     for i in range(groups + 1):
         if i < groups:
@@ -1042,7 +1059,8 @@
     def multiply_theirs(e, q):
         block = other_column(e)
         for d in range(chips):
-            weight_here(e, d, 1 - c, q)
+            for k in shares(q, d):
+                weight_here(e, d, 1 - c, q, k)
         product = jnp.dot(
             mixed[1 - level], weights[block, q], preferred_element_type=jnp.float32
         )
@@ -1070,11 +1088,18 @@
     def token_rows(side):
         return pl.ds(pl.multiple_of(side * tokens, tokens), tokens)
 
-    def finish(column, branch):
+    def finish(column, branch, index, q):
         lanes = lanes_at(column, lane)
-        out_ref[:, lanes] = (
+        result_ref[:, lanes] = (
             hidden_ref[:, lanes].astype(jnp.float32) + gate_ref[:, lanes] * branch
         ).astype(jnp.bfloat16)
+        write_out(column, index, q).start()
+
+    def write_out(column, index, q):
+        lanes = lanes_at(column, lane)
+        return pltpu.make_async_copy(
+            result_ref.at[:, lanes], out_ref.at[:, lanes], out_sem.at[index, q]
+        )
 
     def reduce_part(q):
         for e in range(blocks):
@@ -1087,7 +1112,7 @@
             back(block, q).start()
             ours = token_rows(p)
             branch = total[block, q, ours] + partial_in[block, q, ours].astype(jnp.float32)
-            finish((2 * block + p) * cols + q * lane, branch)
+            finish((2 * block + p) * cols + q * lane, branch, 2 * block + p, q)
 
     def theirs(q):
         if q >= groups - 1:
@@ -1128,35 +1153,37 @@
     own_hidden.wait()
     next_far(3)
     theirs(2)
+    next_far(4)
     ours(1)
-    with jax.named_scope("reduce0"):
+    with jax.named_scope("reduce01"):
         reduce_part(0)
-    next_far(4)
+        reduce_part(1)
     theirs(3)
     ours(2)
-    with jax.named_scope("reduce1"):
-        reduce_part(1)
+    ours(3)
+    with jax.named_scope("reduce2"):
+        reduce_part(2)
+    with jax.named_scope("reduce3a"):
+        pl.when(jnp.logical_not(at_end))(functools.partial(reduce_part, 3))
     theirs(4)
-    ours(3)
     ours(4)
 
     def finish_others(q):
         for block in range(blocks):
             back(block, q).wait_recv()
-            finish((2 * block + 1 - p) * cols + q * lane, incoming[block, q].astype(jnp.float32))
-
-    with jax.named_scope("reduce2"):
-        reduce_part(2)
+            finish(
+                (2 * block + 1 - p) * cols + q * lane,
+                incoming[block, q].astype(jnp.float32), 2 * block + 1 - p, q,
+            )
+
+    with jax.named_scope("reduce3b"):
+        pl.when(at_end)(functools.partial(reduce_part, 3))
     with jax.named_scope("finish01"):
         each_part(0, 2, finish_others)
-    with jax.named_scope("reduce3"):
-        reduce_part(3)
-    with jax.named_scope("finish2"):
-        finish_others(2)
     with jax.named_scope("reduce4"):
         reduce_part(4)
-    with jax.named_scope("finish34"):
-        each_part(3, parts, finish_others)
+    with jax.named_scope("finish2"):
+        each_part(2, parts, finish_others)
 
     for b in range(groups):
         value_swap(b).wait_send()
@@ -1169,18 +1196,27 @@
         for which in range(2):
             to_mate(which, j).wait_send()
 
-    def sent(q):
-        for rising in (True, False):
-            pl.when(starts[rising])(first_hop(rising, q).wait_send)
-            pl.when(passes[rising])(second_hop(rising, q).wait_send)
+    def weight_sent(q):
+        for k in shares(q):
+            for rising in (True, False):
+                pl.when(starts[rising])(first_hop(rising, q, k).wait_send)
+                pl.when(passes[rising])(second_hop(rising, q, k).wait_send)
         for e in range(blocks):
             for d in range(chips):
-                pair_weight(e, d, q).wait_send()
-                if e > 0:
-                    cross_weight(e, d, q).wait_send()
+                for k in shares(q, d):
+                    pair_weight(e, d, q, k).wait_send()
+                    if e > 0:
+                        cross_weight(e, d, q, k).wait_send()
+
+    for q in range(parts):
+        weight_sent(q)
+
+    def sent(q):
         for block in range(blocks):
             part_copy(block, q).wait_send()
             back(block, q).wait_send()
+        for index in range(nt):
+            write_out(index * cols + q * lane, index, q).wait()
 
     each_part(0, parts, sent)
 
@@ -1220,7 +1256,7 @@
         functools.partial(pair_kernel, heads),
         out_shape=jax.ShapeDtypeStruct((tokens, width), jnp.bfloat16),
         in_specs=[pl.BlockSpec(memory_space=pltpu.SMEM)] * 3 + [vmem] * 5 + [hbm] * 5,
-        out_specs=vmem,
+        out_specs=hbm,
         scratch_shapes=[
             pltpu.VMEM((2, frames, rows, columns, inner), jnp.bfloat16),
             pltpu.VMEM((2, 2, frames, rows, columns, half), jnp.bfloat16),
@@ -1235,6 +1271,7 @@
             pltpu.VMEM((blocks, parts, tokens, lane), jnp.bfloat16),
             pltpu.VMEM((blocks, parts, tokens, lane), jnp.bfloat16),
             pltpu.VMEM((tokens, width), jnp.bfloat16),
+            pltpu.VMEM((tokens, width), jnp.bfloat16),
             pltpu.VMEM((2, parts, depth, lane), jnp.bfloat16),
             dma((5,)),
             dma((groups,)),
@@ -1245,11 +1282,11 @@
             dma((4, groups)),
             dma((4, groups)),
             dma((4, groups)),
-            dma((2, parts)),
-            dma((2, 2, parts)),
-            dma((max(blocks - 1, 1), chips, parts)),
-            dma((blocks, chips, parts)),
-            dma((blocks, 2 * chips, parts)),
+            dma((2, parts + 1)),
+            dma((2, 2, parts + 1)),
+            dma((max(blocks - 1, 1), chips, parts + 1)),
+            dma((blocks, chips, parts + 1)),
+            dma((blocks, 2 * chips, parts + 1)),
             dma((groups // 2,)),
             dma((groups // 2,)),
             dma((2, groups // 2)),
@@ -1258,6 +1295,7 @@
             dma((blocks, parts)),
             dma((blocks, parts)),
             dma((blocks, parts)),
+            dma((nt, parts)),
         ],
         compiler_params=pltpu.CompilerParams(
             collective_id=0, has_side_effects=True, vmem_limit_bytes=60 * 1024 * 1024

time: 126 us -> 123 us (0.976)
  the two profiles are of different devices: /device:TPU:11 before, /device:TPU:0 now
where the time goes in v3:
time: 123 us
  Pallas kernels  120 us (98%)
  local copies, waits for them, and re-layouts  2.46 us (2%)
    pallas_call x1, Pallas kernels, pair_shards(): pl.pallas_call(functools.partial(pair_kernel, heads), out_shape=jax.Shape...  120 us

profile of v3, /device:TPU:0, one launch (start us, length us, event | category | flops | bytes accessed | tf_op | source)
XLA Modules:
  0.0 122.9 jit_solution(1423058353300096765)
XLA Ops:
  0.0 120.4 %shard_map.127 = bf16[128,5120]{1,0:T(8,128)(2,1)} custom-call(s32[40]{0:T(128)} %time_ref.1, s32[40]{0:T(128)} %rows_ref.1, s32[40]{0:T(128)} %cols_ref.1, f32[1,5120]{1,0:T(1,128)} %bitcast.7, f32[1,5120]{1,0:T(1,128)} %bitcast.8, s32[64,2]{1,0:T(8,128)} %constant.4.clone.query_place_ref, s32[3,384]{1,0:T(4,128)} %constant.5.clone.key_place_ref, ...), custom_call_target="tpu_custom_call" | custom-call | tf_op jit(solution)/shard_map/pallas_call | solution.py:1255
  120.4 2.5 %copy.15 = bf16[2,2,32,5120]{3,2,1,0:T(8,128)(2,1)} copy(bf16[2,2,32,5120]{3,2,1,0:T(8,128)(2,1)} %bitcast.5) | data formatting | bytes 2621440

commit v4 on v3

--- a/solution.py
+++ b/solution.py
@@ -773,6 +773,7 @@
         own_value(b).start()
     send_far(0, True)
     send_far(0, False)
+    send_far(1, False)
     send_cross(0)
     for q in range(parts):
         keep_weight(q).start()
@@ -1015,11 +1016,11 @@
         "early": lambda q: relay_far(q, False),
     }
     plan = {i: [] for i in range(groups + 1)}
-    plan[0] += [("mid", 1), ("end", 1), ("cross", 1), ("out", 0)]
-    plan[1] += [("mid", 2), ("end0", 2), ("cross", 2), ("out0", 1)]
-    plan[2] += [("mid", 3), ("end1", 2), ("cross", 3), ("out1", 1)]
-    plan[3] += [("in", 0), ("end0", 3), ("out0", 2), ("cross", 4), ("early", 0), ("early", 1)]
-    plan[groups] += [("mid", 4), ("in", 1), ("end1", 3), ("end", 4), ("out1", 2), ("out", 3), ("late", 0)]
+    plan[0] += [("mid", 2), ("end", 1), ("cross", 1), ("out", 0)]
+    plan[1] += [("mid", 3), ("end0", 2), ("cross", 2), ("out0", 1)]
+    plan[2] += [("end1", 2), ("cross", 3), ("out1", 1)]
+    plan[3] += [("in", 0), ("mid", 4), ("end0", 3), ("out0", 2), ("cross", 4), ("early", 0), ("early", 1)]
+    plan[groups] += [("in", 1), ("end1", 3), ("end", 4), ("out1", 2), ("out", 3), ("late", 0)]
     plan[groups] += [("cross", q) for q in range(5, parts)]
     for i in range(groups + 1):
         if i < groups:

time: 123 us -> 122 us (level)
  no operation moved by 1% of the time
where the time goes in v4:
time: 122 us
  Pallas kernels  119 us (98%)
  local copies, waits for them, and re-layouts  2.46 us (2%)
    pallas_call x1, Pallas kernels, pair_shards(): pl.pallas_call(functools.partial(pair_kernel, heads), out_shape=jax.Shape...  119 us
    unnamed x1, local copies, waits for them, and re-layouts  2.46 us

profile of v4, /device:TPU:0, one launch (start us, length us, event | category | flops | bytes accessed | tf_op | source)
XLA Modules:
  0.0 122.0 jit_solution(6942739574559813335)
XLA Ops:
  0.0 119.5 %shard_map.127 = bf16[128,5120]{1,0:T(8,128)(2,1)} custom-call(s32[40]{0:T(128)} %time_ref.1, s32[40]{0:T(128)} %rows_ref.1, s32[40]{0:T(128)} %cols_ref.1, f32[1,5120]{1,0:T(1,128)} %bitcast.7, f32[1,5120]{1,0:T(1,128)} %bitcast.8, s32[64,2]{1,0:T(8,128)} %constant.4.clone.query_place_ref, s32[3,384]{1,0:T(4,128)} %constant.5.clone.key_place_ref, ...), custom_call_target="tpu_custom_call" | custom-call | tf_op jit(solution)/shard_map/pallas_call | solution.py:1256
  119.5 2.5 %copy.15 = bf16[2,2,32,5120]{3,2,1,0:T(8,128)(2,1)} copy(bf16[2,2,32,5120]{3,2,1,0:T(8,128)(2,1)} %bitcast.5) | data formatting | bytes 2621440

commit v5 on v4

--- a/solution.py
+++ b/solution.py
@@ -774,6 +774,7 @@
     send_far(0, True)
     send_far(0, False)
     send_far(1, False)
+    send_far(1, True)
     send_cross(0)
     for q in range(parts):
         keep_weight(q).start()
@@ -1016,7 +1017,7 @@
         "early": lambda q: relay_far(q, False),
     }
     plan = {i: [] for i in range(groups + 1)}
-    plan[0] += [("mid", 2), ("end", 1), ("cross", 1), ("out", 0)]
+    plan[0] += [("mid", 2), ("cross", 1), ("out", 0)]
     plan[1] += [("mid", 3), ("end0", 2), ("cross", 2), ("out0", 1)]
     plan[2] += [("end1", 2), ("cross", 3), ("out1", 1)]
     plan[3] += [("in", 0), ("mid", 4), ("end0", 3), ("out0", 2), ("cross", 4), ("early", 0), ("early", 1)]

time: 122 us -> 122 us (level)
  no operation moved by 1% of the time
where the time goes in v5:
time: 122 us
  Pallas kernels  119 us (98%)
  local copies, waits for them, and re-layouts  2.46 us (2%)
    pallas_call x1, Pallas kernels, pair_shards(): pl.pallas_call(functools.partial(pair_kernel, heads), out_shape=jax.Shape...  119 us
    unnamed x1, local copies, waits for them, and re-layouts  2.46 us

profile of v5, /device:TPU:0, one launch (start us, length us, event | category | flops | bytes accessed | tf_op | source)
XLA Modules:
  0.0 122.0 jit_solution(11795868419322765430)
XLA Ops:
  0.0 119.5 %shard_map.127 = bf16[128,5120]{1,0:T(8,128)(2,1)} custom-call(s32[40]{0:T(128)} %time_ref.1, s32[40]{0:T(128)} %rows_ref.1, s32[40]{0:T(128)} %cols_ref.1, f32[1,5120]{1,0:T(1,128)} %bitcast.7, f32[1,5120]{1,0:T(1,128)} %bitcast.8, s32[64,2]{1,0:T(8,128)} %constant.4.clone.query_place_ref, s32[3,384]{1,0:T(4,128)} %constant.5.clone.key_place_ref, ...), custom_call_target="tpu_custom_call" | custom-call | tf_op jit(solution)/shard_map/pallas_call | solution.py:1257
  119.5 2.5 %copy.15 = bf16[2,2,32,5120]{3,2,1,0:T(8,128)(2,1)} copy(bf16[2,2,32,5120]{3,2,1,0:T(8,128)(2,1)} %bitcast.5) | data formatting | bytes 2621440
